TPU v7x, 32 devices: a whole 2x2x4 slice. The times are simulated.
32 devices in a mesh: dp: 8 (over z, x), rep: 4 (over y, core).
Axes of the slice: x: 2, y: 2, z: 4, core: 2. Of those that a mesh axis runs over, the one named last changes fastest.
Arguments:
- token_inputs: bfloat16 [16384, 2048], P(('dp', 'rep')), may hold values from -12 to 12
- cotangent: bfloat16 [16384, 2048], P(('dp', 'rep')), may hold values from -6 to 6
- gate_preact: bfloat16 [16384, 768], P(('dp', 'rep')), may hold values from -6 to 6
- up_preact: bfloat16 [16384, 768], P(('dp', 'rep')), may hold values from -6 to 6
- down_weight: bfloat16 [2, 768, 2048], P(None, None, 'dp'), may hold values from -0.21875 to 0.21875
- block_expert: int32 [128], P(('dp', 'rep')), may hold values from 0 to 1
- block_count: int32 [128], P(('dp', 'rep')), may hold values from 1 to 128, as said below
Outputs:
- update: bfloat16 [2, 3, 768, 2048], P(None, None, None, 'dp')
Inputs may be any that keep to these rules, and one draw needn't show every extreme that they name: `block_count`: live rows of a block, at most 128; in every draw some block is full.
All inputs are finite; a program needn't handle non-finite values.
Results may differ from a plain program's by a relative error of at most 0.02.
Values may be sent and summed in bfloat16 or wider, within the bound.
A program may use at most 128 MiB of HBM per device.

v0:
```python
import math
import jax
import jax.numpy as jnp
from jax import lax
from jax.sharding import PartitionSpec as P

D = 2048
ITERS = 2
ns_first = 3.4445
ns_second = -4.775
ns_third = 2.0315
norm_eps = 1e-07


def whole_sweeps(matrix, column_width, groups_all, sweeps, scale):
    hidden_width = matrix.shape[0]
    group = math.gcd(8, groups_all)
    current = matrix
    result = None
    for sweep in range(sweeps):

        def add_group(index, total):
            cols = lax.dynamic_slice_in_dim(
                current, index * group * column_width, group * column_width, 1
            )
            cols = cols.reshape(hidden_width, group, column_width)
            term = jnp.einsum(
                "fnd,gnd->nfg", cols, cols, preferred_element_type=jnp.float32
            ).astype(jnp.bfloat16)
            return total + jnp.sum(lax.optimization_barrier(term).astype(jnp.float32), axis=0)

        gram = lax.fori_loop(
            0, groups_all // group, add_group, jnp.zeros((hidden_width, hidden_width), jnp.float32)
        )
        gram_half = gram.astype(jnp.bfloat16)
        squared = jnp.dot(gram_half, gram_half, preferred_element_type=jnp.float32)
        poly = (ns_second * gram + ns_third * squared).astype(jnp.bfloat16)
        newer = ns_first * current.astype(jnp.float32) + jnp.dot(
            poly, current, preferred_element_type=jnp.float32
        )
        if sweep + 1 < sweeps:
            current = newer.astype(jnp.bfloat16)
        else:
            result = (scale * newer).astype(jnp.bfloat16)
    return result


def per_device(
    token_inputs, cotangent, gate_preact, up_preact, down_weight, block_expert, block_count
):
    blocks = block_count.shape[0]
    rows_here = token_inputs.shape[0]
    hidden_width = gate_preact.shape[1]
    width = token_inputs.shape[1]
    block_rows = rows_here // blocks
    experts_here = down_weight.shape[0]
    row_place = jnp.arange(rows_here, dtype=jnp.int32) % block_rows
    row_count = jnp.repeat(block_count, block_rows, total_repeat_length=rows_here)
    row_expert = jnp.repeat(block_expert, block_rows, total_repeat_length=rows_here)
    live_rows = row_place < row_count
    masked = jnp.where(live_rows[:, None], cotangent, jnp.zeros_like(cotangent))
    gate = gate_preact.astype(jnp.float32)
    upper = up_preact.astype(jnp.float32)
    sigmoid_gate = jax.nn.sigmoid(gate)
    hidden = (gate * sigmoid_gate * upper).astype(jnp.bfloat16)
    selector = (row_expert[None, :] == jnp.arange(experts_here, dtype=jnp.int32)[:, None]).astype(
        jnp.bfloat16
    )
    masked_each = masked[None, :, :] * selector[:, :, None]
    weights_all = lax.all_gather(down_weight, "dp", axis=2, tiled=True)
    back = jnp.einsum("erd,efd->rf", masked_each, weights_all, preferred_element_type=jnp.float32)
    grad_gate = (back * upper * sigmoid_gate * (1.0 + gate * (1.0 - sigmoid_gate))).astype(
        jnp.bfloat16
    )
    grad_up = (back * gate * sigmoid_gate).astype(jnp.bfloat16)
    gate_up = jnp.concatenate([grad_gate, grad_up], axis=1)
    gate_up_each = gate_up[None, :, :] * selector[:, :, None]
    hidden_each = hidden[None, :, :] * selector[:, :, None]
    input_part = jnp.einsum(
        "erf,rd->efd", gate_up_each, token_inputs, preferred_element_type=jnp.float32
    )
    output_part = jnp.einsum("erf,rd->efd", hidden_each, masked, preferred_element_type=jnp.float32)
    partial_value = jnp.concatenate(
        [input_part.reshape(experts_here, 2, hidden_width, width), output_part[:, None]], axis=1
    )
    partial_half = partial_value.astype(jnp.bfloat16)
    terms = lax.optimization_barrier(partial_half).astype(jnp.float32)
    grad = lax.psum_scatter(
        terms.astype(jnp.bfloat16), "dp", scatter_dimension=3, tiled=True
    ).astype(jnp.float32)
    grad = lax.psum(grad.astype(jnp.bfloat16), "rep").astype(jnp.float32)
    squares = lax.psum(jnp.sum(grad * grad, axis=(2, 3)), "dp")
    current = (grad / (jnp.sqrt(squares) + norm_eps)[:, :, None, None]).astype(jnp.bfloat16)
    column_width = current.shape[3]
    scale = jnp.sqrt(jnp.float32(D))
    result = None
    n_dp = lax.axis_size("dp")
    matrices = experts_here * 3
    flat = current.reshape(matrices, hidden_width, column_width)
    padding = jnp.zeros((n_dp - matrices, hidden_width, column_width), jnp.bfloat16)
    outbound = jnp.concatenate([flat, padding], axis=0)
    owned = lax.all_to_all(outbound, "dp", split_axis=0, concat_axis=2, tiled=True)
    finished = whole_sweeps(owned[0], column_width, n_dp, ITERS, scale)
    returned = lax.all_to_all(finished[None], "dp", split_axis=2, concat_axis=0, tiled=True)
    result = returned[:matrices].reshape(experts_here, 3, hidden_width, column_width)
    return result


def solution(mesh):
    placed = (
        P(("dp", "rep"), None),
        P(("dp", "rep"), None),
        P(("dp", "rep"), None),
        P(("dp", "rep"), None),
        P(None, None, "dp"),
        P(("dp", "rep")),
        P(("dp", "rep")),
    )
    return jax.shard_map(
        per_device, mesh=mesh, in_specs=placed, out_specs=P(None, None, None, "dp"), check_vma=False
    )
```

profile of v0, /device:TPU:0, one launch (start us, length us, event | category | flops | bytes accessed | tf_op | source)
XLA Modules:
  0.0 795.3 jit_solution(15564926438498596758)
XLA Ops:
  6.5 0.0 copy-start
  6.5 0.0 all-gather.2.cloned.1.call-start
  6.5 0.7 all-gather.2.cloned.1.call-update
  7.3 0.0 reduce-scatter.2.cloned.1.call-start
  7.3 1.4 fusion.46
  8.7 2.5 fusion.34
  11.2 1.4 fusion.45
  12.6 2.5 select_select_fusion
  15.2 3.1 broadcast_select_fusion
  18.3 93.3 %all-gather.2.cloned.1.call-done = bf16[2,768,2048]{2,1,0:T(8,128)(2,1)} async-done(((bf16[2,768,256]{2,1,0:T(8,128)(2,1)}), bf16[2,768,2048]{2,1,0:T(8,128)(2,1)}) %all-gather.2.cloned.1.call-update) | async-done | bytes 6291472 | tf_op jit(solution)/shard_map/all_gather | solution.py:70
  111.6 7.8 fusion.15
  119.4 1.3 pad_maximum_fusion.1
  120.7 2.6 copy.31
  123.3 1.2 copy.32
  124.5 0.0 copy-start.3
  124.5 5.5 convert_bitcast_fusion
  129.9 0.0 copy-done
  130.0 0.0 copy-done.3
  130.0 6.9 convolution_convert_fusion
  136.9 10.4 %pad_maximum_fusion = bf16[2,3,768,2048]{3,2,1,0:T(8,128)(2,1)} fusion(bf16[2,1,768,2048]{3,2,1,0:T(8,128)(2,1)S(1)} %convert_bitcast_fusion, bf16[2,2,768,2048]{3,2,1,0:T(8,128)(2,1)S(1)} %bitcast.77), kind=kLoop, calls=%fused_computation | loop fusion | flops 9437184 | bytes 37748736 | tf_op jit(solution)/shard_map/concatenate | solution.py:83
  147.3 0.0 reduce-scatter.2.cloned.1.call-update
  147.4 0.0 all-reduce.3.cloned.1.call-start
  147.4 308.6 %reduce-scatter.2.cloned.1.call-done = bf16[2,3,768,256]{3,2,1,0:T(8,128)(2,1)} async-done(((bf16[2,3,768,2048]{3,2,1,0:T(8,128)(2,1)}), bf16[2,3,768,256]{3,2,1,0:T(8,128)(2,1)}) %reduce-scatter.2.cloned.1.call-update) | async-done | bytes 2359312 | tf_op jit(solution)/shard_map/reduce_scatter | solution.py:88
  456.1 0.0 all-reduce.3.cloned.1.call-update
  456.1 57.2 %all-reduce.3.cloned.1.call-done = bf16[2,3,768,256]{3,2,1,0:T(8,128)(2,1)} async-done(((bf16[2,3,768,256]{3,2,1,0:T(8,128)(2,1)}), bf16[2,3,768,256]{3,2,1,0:T(8,128)(2,1)}) %all-reduce.3.cloned.1.call-update) | async-done | bytes 2359312 | tf_op jit(solution)/shard_map/psum | solution.py:91
  513.2 0.0 copy-start.2
  513.2 2.5 fusion
  515.7 21.3 %psum.15 = f32[2,3]{1,0:T(2,128)S(1)} all-reduce(f32[2,3]{1,0:T(2,128)S(1)} %fusion), channel_id=1, replica_groups=mesh['dp'=8,'rep'=4] {'dp'}, use_global_device_ids=true, to_apply=%region_3.5 | all-reduce | flops 6 | bytes 48 | tf_op jit(solution)/shard_map/psum | solution.py:92
  537.0 0.0 copy-done.2
  537.0 0.9 fusion.1
  538.0 0.2 concatenate.18
  538.2 70.2 %all_to_all.30 = bf16[8,768,256]{2,1,0:T(8,128)(2,1)} all-to-all(bf16[8,768,256]{2,1,0:T(8,128)(2,1)S(1)} %concatenate.18), channel_id=1, replica_groups=mesh['dp'=8,'rep'=4] {'dp'}, dimensions={0} | all-to-all | bytes 6291456 | tf_op jit(solution)/shard_map/all_to_all | solution.py:102
  608.4 5.5 convolution_convert_fusion.2
  613.9 2.7 convert_reduce_fusion.1
  616.6 3.2 copy.34
  619.8 3.0 copy.35
  622.8 9.3 %add_convert_fusion = bf16[768,2048]{1,0:T(8,128)(2,1)} fusion(bf16[768,2048]{1,0:T(8,128)(2,1)} %copy.35, bf16[768,2048]{0,1:T(8,128)(2,1)S(1)} %bitcast.76, f32[768,768]{1,0:T(8,128)} %convert_reduce_fusion.1), kind=kOutput, calls=%fused_computation.7 | convolution fusion | flops 3331129344 | bytes 11796480 | tf_op jit(solution)/shard_map/dot_general | solution.py:38
  632.1 5.5 convolution_convert_fusion.1
  637.6 2.7 convert_reduce_fusion
  640.4 8.7 %fusion.8 = bf16[1,768,2048]{2,1,0:T(8,128)(2,1)S(1)} fusion(bf16[768,2048]{1,0:T(8,128)(2,1)} %add_convert_fusion, f32[768,768]{1,0:T(8,128)} %convert_reduce_fusion), kind=kOutput, calls=%fused_computation.19 | convolution fusion | flops 3332702208 | bytes 8650752 | tf_op jit(solution)/shard_map/dot_general | solution.py:38
  649.1 11.2 %copy.38 = bf16[1,768,2048]{1,0,2:T(2,128)(2,1)} copy(bf16[1,768,2048]{2,1,0:T(8,128)(2,1)S(1)} %fusion.8) | data formatting | bytes 6291456 | tf_op jit(solution)/shard_map/broadcast_in_dim | solution.py:104
  660.3 0.5 broadcast.198
  660.8 33.5 %reduce.3 = bf16[2048,768]{1,0:T(8,128)(2,1)} reduce(bf16[2048,1,768]{2,1,0:T(2,128)(2,1)} %bitcast.73, bf16[]{:T(256)} %broadcast.198), dimensions={1}, to_apply=%bitcast.67.reduce_sub_computation | reduce | bytes 6291458
  694.3 4.6 reshape.141
  699.0 72.8 %all_to_all.31 = bf16[8,2,98304]{2,1,0:T(2,128)(2,1)} all-to-all(bf16[8,2,98304]{2,1,0:T(2,128)(2,1)S(1)} %reshape.141), channel_id=1, replica_groups=mesh['dp'=8,'rep'=4] {'dp'}, dimensions={0} | all-to-all | bytes 6291456 | tf_op jit(solution)/shard_map/all_to_all | solution.py:104
  771.8 7.8 reshape.142
  779.6 3.3 copy.40
  782.9 0.0 copy-start.1
  782.9 1.6 slice.46
  784.5 4.3 copy.39
  788.7 0.0 copy-done.1
  (2 shorter events, 0.0 us)
Async XLA Ops:
  6.5 123.4 %copy-start = (bf16[512,2048]{1,0:T(8,128)(2,1)S(1)}, bf16[512,2048]{1,0:T(8,128)(2,1)}, u32[]{:S(2)}) copy-start(bf16[512,2048]{1,0:T(8,128)(2,1)} %param.13) | copy-start | bytes 6291460
  6.5 105.1 %all-gather.2.cloned.1.call-start = ((), (), s32[]{:S(2)}) async-start(), calls=%async_computation.3 | async-start | bytes 7077888 | tf_op jit(solution)/shard_map/all_gather | solution.py:70
  7.3 448.8 %reduce-scatter.2.cloned.1.call-start = ((), (), s32[]{:S(2)}) async-start(), calls=%async_computation.4 | async-start | bytes 21233664 | tf_op jit(solution)/shard_map/reduce_scatter | solution.py:88
  124.5 5.5 copy-start.3
  147.4 365.9 %all-reduce.3.cloned.1.call-start = ((), (), s32[]{:S(2)}) async-start(), calls=%async_computation.5 | async-start | bytes 4718592 | tf_op jit(solution)/shard_map/psum | solution.py:91
  513.2 23.8 %copy-start.2 = (bf16[2,3,768,256]{3,2,1,0:T(8,128)(2,1)S(1)}, bf16[2,3,768,256]{3,2,1,0:T(8,128)(2,1)}, u32[]{:S(2)}) copy-start(bf16[2,3,768,256]{3,2,1,0:T(8,128)(2,1)} %all-reduce.3.cloned.1.call-done) | copy-start | bytes 7077892
  782.9 5.9 copy-start.1
Sparse Core Ops, SparseCore 0:
  9.4 102.1 all-gather.1
  147.5 308.5 reduce-scatter.1
  458.4 54.7 all-reduce.2
where the time goes:
time: 796 us; the launch traced here: 795 us
  waiting for transfers between devices  460 us (58%)
  blocking collectives  164 us (21%)
  other arithmetic  62.2 us (8%)
  matrix products  49.3 us (6%)
  local copies, waits for them, and re-layouts  46.3 us (6%)
  between operations  13.2 us (2%)
    reduce_scatter x1, waiting for transfers between devices, per_device(): lax.psum_scatter(terms.astype(jnp.bfloat16), 'dp', scatter_dimension=3, t...  309 us
    all_gather x1, waiting for transfers between devices, per_device(): weights_all = lax.all_gather(down_weight, 'dp', axis=2, tiled=True)  93.3 us
    all_to_all x1, blocking collectives, per_device(): lax.all_to_all(finished[None], 'dp', split_axis=2, concat_axis=0, tiled=T...  72.8 us
    all_to_all x1, blocking collectives, per_device(): lax.all_to_all(outbound, 'dp', split_axis=0, concat_axis=2, tiled=True)  70.2 us
    psum x1, waiting for transfers between devices, per_device(): grad = lax.psum(grad.astype(jnp.bfloat16), 'rep').astype(jnp.float32)  57.2 us
    unnamed x1, other arithmetic  33.5 us
    psum x1, blocking collectives, per_device(): squares = lax.psum(jnp.sum(grad * grad, axis=(2, 3)), 'dp')  21.3 us
    dot_general x2, matrix products, whole_sweeps(): jnp.dot(poly, current, preferred_element_type=jnp.float32)  18 us
  transfers between devices with their start and end apart: 3, of which 3 were waited for; matrix products, arithmetic and copies ran while one was open for 1% of the time, Pallas kernels for 0%

commit v1 on v0

--- a/solution.py
+++ b/solution.py
@@ -67,7 +67,12 @@
         jnp.bfloat16
     )
     masked_each = masked[None, :, :] * selector[:, :, None]
-    weights_all = lax.all_gather(down_weight, "dp", axis=2, tiled=True)
+    ring = [down_weight]
+    for hop in range(7):
+        ring.append(lax.ppermute(ring[-1], "dp", [(dev, (dev + 1) % 8) for dev in range(8)]))
+    weights_all = jnp.roll(
+        jnp.concatenate(ring[::-1], axis=2), (lax.axis_index("dp") + 1) * ring[0].shape[2], axis=2
+    )
     back = jnp.einsum("erd,efd->rf", masked_each, weights_all, preferred_element_type=jnp.float32)
     grad_gate = (back * upper * sigmoid_gate * (1.0 + gate * (1.0 - sigmoid_gate))).astype(
         jnp.bfloat16

time: 796 us -> 838 us (1.053)
  waiting for transfers between devices: 460 us -> 491 us
  local copies, waits for them, and re-layouts: 46.3 us -> 57.7 us
    ppermute x0 -> x7, waiting for transfers between devices: none -> 127 us  [per_device(): lax.ppermute(ring[-1], 'dp', [(dev, (dev + 1) % 8) for dev in range(8)])]
    all_gather x1 -> x0, waiting for transfers between devices: 93.3 us -> none  [per_device(): weights_all = lax.all_gather(down_weight, 'dp', axis=2, tiled=True)]
    unnamed x12 -> x51, local copies, waits for them, and re-layouts: 16.2 us -> 27.5 us
  transfers between devices with their start and end apart: 3 -> 9, of which waited for: 3 -> 9; matrix products, arithmetic and copies ran while one was open for 1% -> 1% of each run, Pallas kernels for 0% -> 0%
where the time goes in v1:
time: 838 us; the launch traced here: 837 us
  waiting for transfers between devices  491 us (59%)
  blocking collectives  164 us (20%)
  other arithmetic  61.1 us (7%)
  local copies, waits for them, and re-layouts  57.7 us (7%)
  matrix products  45.5 us (5%)
  between operations  13.8 us (2%)
    reduce_scatter x1, waiting for transfers between devices, per_device(): lax.psum_scatter(terms.astype(jnp.bfloat16), 'dp', scatter_dimension=3, t...  307 us
    ppermute x7, waiting for transfers between devices, per_device(): lax.ppermute(ring[-1], 'dp', [(dev, (dev + 1) % 8) for dev in range(8)])  127 us
    all_to_all x1, blocking collectives, per_device(): lax.all_to_all(finished[None], 'dp', split_axis=2, concat_axis=0, tiled=T...  72.8 us
    all_to_all x1, blocking collectives, per_device(): lax.all_to_all(outbound, 'dp', split_axis=0, concat_axis=2, tiled=True)  70.2 us
    psum x1, waiting for transfers between devices, per_device(): grad = lax.psum(grad.astype(jnp.bfloat16), 'rep').astype(jnp.float32)  57.1 us
    unnamed x1, other arithmetic  33.6 us
    unnamed x51, local copies, waits for them, and re-layouts  27.5 us
    psum x1, blocking collectives, per_device(): squares = lax.psum(jnp.sum(grad * grad, axis=(2, 3)), 'dp')  21.3 us
  transfers between devices with their start and end apart: 9, of which 9 were waited for; matrix products, arithmetic and copies ran while one was open for 1% of the time, Pallas kernels for 0%

profile of v1, /device:TPU:0, one launch (start us, length us, event | category | flops | bytes accessed | tf_op | source)
XLA Modules:
  0.0 836.8 jit_solution(1983767858085236049)
XLA Ops:
  6.5 3.0 collective-permute-start
  9.5 20.8 %collective-permute-done = bf16[2,768,256]{2,1,0:T(8,128)(2,1)S(1)} collective-permute-done((bf16[2,768,256]{2,1,0:T(8,128)(2,1)}, bf16[2,768,256]{2,1,0:T(8,128)(2,1)S(1)}, u32[]{:S(2)}, u32[]{:S(2)}) %collective-permute-start) | collective-permute-done | bytes 786464 | tf_op jit(solution)/shard_map/ppermute | solution.py:72
  30.3 21.4 %collective-permute-done.1 = bf16[2,768,256]{2,1,0:T(8,128)(2,1)S(1)} collective-permute-done((bf16[2,768,256]{2,1,0:T(8,128)(2,1)S(1)}, bf16[2,768,256]{2,1,0:T(8,128)(2,1)S(1)}, u32[]{:S(2)}, u32[]{:S(2)}) %collective-permute-start.1) | collective-permute-done | bytes 786464 | tf_op jit(solution)/shard_map/ppermute | solution.py:72
  51.7 0.9 copy-done.4
  52.6 20.5 %collective-permute-done.2 = bf16[2,768,256]{2,1,0:T(8,128)(2,1)S(1)} collective-permute-done((bf16[2,768,256]{2,1,0:T(8,128)(2,1)S(1)}, bf16[2,768,256]{2,1,0:T(8,128)(2,1)S(1)}, u32[]{:S(2)}, u32[]{:S(2)}) %collective-permute-start.2) | collective-permute-done | bytes 786464 | tf_op jit(solution)/shard_map/ppermute | solution.py:72
  73.1 0.9 copy-done.6
  74.0 19.7 %collective-permute-done.3 = bf16[2,768,256]{2,1,0:T(8,128)(2,1)S(1)} collective-permute-done((bf16[2,768,256]{2,1,0:T(8,128)(2,1)S(1)}, bf16[2,768,256]{2,1,0:T(8,128)(2,1)S(1)}, u32[]{:S(2)}, u32[]{:S(2)}) %collective-permute-start.3) | collective-permute-done | bytes 786464 | tf_op jit(solution)/shard_map/ppermute | solution.py:72
  93.7 0.9 copy-done.8
  94.6 18.8 %collective-permute-done.4 = bf16[2,768,256]{2,1,0:T(8,128)(2,1)S(1)} collective-permute-done((bf16[2,768,256]{2,1,0:T(8,128)(2,1)S(1)}, bf16[2,768,256]{2,1,0:T(8,128)(2,1)S(1)}, u32[]{:S(2)}, u32[]{:S(2)}) %collective-permute-start.4) | collective-permute-done | bytes 786464 | tf_op jit(solution)/shard_map/ppermute | solution.py:72
  113.4 0.9 copy-done.10
  114.3 1.5 fusion.47
  115.8 2.6 select_select_fusion
  118.4 1.5 fusion.48
  119.9 12.5 %collective-permute-done.5 = bf16[2,768,256]{2,1,0:T(8,128)(2,1)} collective-permute-done((bf16[2,768,256]{2,1,0:T(8,128)(2,1)S(1)}, bf16[2,768,256]{2,1,0:T(8,128)(2,1)}, u32[]{:S(2)}, u32[]{:S(2)}) %collective-permute-start.5) | collective-permute-done | bytes 786464 | tf_op jit(solution)/shard_map/ppermute | solution.py:72
  132.4 2.5 fusion.35
  135.0 1.9 broadcast_select_fusion
  136.9 13.0 %collective-permute-done.6 = bf16[2,768,256]{2,1,0:T(8,128)(2,1)} collective-permute-done((bf16[2,768,256]{2,1,0:T(8,128)(2,1)}, bf16[2,768,256]{2,1,0:T(8,128)(2,1)}, u32[]{:S(2)}, u32[]{:S(2)}) %collective-permute-start.6) | collective-permute-done | bytes 786464 | tf_op jit(solution)/shard_map/ppermute | solution.py:72
  149.8 1.2 constant_dynamic-update-slice_fusion.15
  151.1 1.3 constant_dynamic-update-slice_fusion.14
  152.4 0.1 constant_dynamic-update-slice_fusion.13
  152.5 0.1 constant_dynamic-update-slice_fusion.12
  152.9 0.1 constant_dynamic-update-slice_fusion.9
  153.0 0.7 copy-done.3
  153.8 1.2 constant_dynamic-update-slice_fusion.7
  155.0 1.2 constant_dynamic-update-slice_fusion.6
  156.3 0.1 constant_dynamic-update-slice_fusion.5
  156.4 0.1 constant_dynamic-update-slice_fusion.4
  156.6 0.1 constant_dynamic-update-slice_fusion.2
  156.7 0.1 constant_dynamic-update-slice_fusion.1
  156.8 0.1 constant_dynamic-update-slice_fusion
  157.0 0.7 copy-done.14
  157.6 0.2 copy-done.15
  157.9 4.2 fusion.16
  162.1 1.3 pad_maximum_fusion.1
  163.3 2.6 copy.31
  166.0 1.1 copy.32
  167.1 5.5 convert_bitcast_fusion
  172.6 6.9 convolution_convert_fusion
  179.5 10.4 %pad_maximum_fusion = bf16[2,3,768,2048]{3,2,1,0:T(8,128)(2,1)} fusion(bf16[2,1,768,2048]{3,2,1,0:T(8,128)(2,1)S(1)} %convert_bitcast_fusion, bf16[2,2,768,2048]{3,2,1,0:T(8,128)(2,1)S(1)} %bitcast.76), kind=kLoop, calls=%fused_computation | loop fusion | flops 9437184 | bytes 37748736 | tf_op jit(solution)/shard_map/concatenate | solution.py:88
  190.0 0.2 all-reduce.3.cloned.1.call-start
  190.2 307.1 %reduce-scatter.2.cloned.1.call-done = bf16[2,3,768,256]{3,2,1,0:T(8,128)(2,1)} async-done(((bf16[2,3,768,2048]{3,2,1,0:T(8,128)(2,1)}), bf16[2,3,768,256]{3,2,1,0:T(8,128)(2,1)}) %reduce-scatter.2.cloned.1.call-update) | async-done | bytes 2359312 | tf_op jit(solution)/shard_map/reduce_scatter | solution.py:93
  497.4 57.1 %all-reduce.3.cloned.1.call-done = bf16[2,3,768,256]{3,2,1,0:T(8,128)(2,1)} async-done(((bf16[2,3,768,256]{3,2,1,0:T(8,128)(2,1)}), bf16[2,3,768,256]{3,2,1,0:T(8,128)(2,1)}) %all-reduce.3.cloned.1.call-update) | async-done | bytes 2359312 | tf_op jit(solution)/shard_map/psum | solution.py:96
  554.5 2.5 fusion.2
  557.0 21.3 %psum.15 = f32[2,3]{1,0:T(2,128)S(1)} all-reduce(f32[2,3]{1,0:T(2,128)S(1)} %fusion.2), channel_id=1, replica_groups=mesh['dp'=8,'rep'=4] {'dp'}, use_global_device_ids=true, to_apply=%region_3.5 | all-reduce | flops 6 | bytes 48 | tf_op jit(solution)/shard_map/psum | solution.py:97
  578.3 0.9 fusion.3
  579.3 0.2 concatenate.25
  579.5 70.2 %all_to_all.30 = bf16[8,768,256]{2,1,0:T(8,128)(2,1)} all-to-all(bf16[8,768,256]{2,1,0:T(8,128)(2,1)S(1)} %concatenate.25), channel_id=1, replica_groups=mesh['dp'=8,'rep'=4] {'dp'}, dimensions={0} | all-to-all | bytes 6291456 | tf_op jit(solution)/shard_map/all_to_all | solution.py:107
  649.7 5.5 convolution_convert_fusion.2
  655.2 2.7 convert_reduce_fusion.1
  657.9 3.2 copy.34
  661.1 3.0 copy.35
  664.1 9.3 %add_convert_fusion = bf16[768,2048]{1,0:T(8,128)(2,1)} fusion(bf16[768,2048]{1,0:T(8,128)(2,1)} %copy.35, bf16[768,2048]{0,1:T(8,128)(2,1)S(1)} %bitcast.75, f32[768,768]{1,0:T(8,128)} %convert_reduce_fusion.1), kind=kOutput, calls=%fused_computation.7 | convolution fusion | flops 3331129344 | bytes 11796480 | tf_op jit(solution)/shard_map/dot_general | solution.py:38
  673.4 5.5 convolution_convert_fusion.1
  678.9 2.7 convert_reduce_fusion
  681.6 8.6 %fusion.9 = bf16[1,768,2048]{2,1,0:T(8,128)(2,1)S(1)} fusion(bf16[768,2048]{1,0:T(8,128)(2,1)} %add_convert_fusion, f32[768,768]{1,0:T(8,128)} %convert_reduce_fusion), kind=kOutput, calls=%fused_computation.20 | convolution fusion | flops 3332702208 | bytes 8650752 | tf_op jit(solution)/shard_map/dot_general | solution.py:38
  690.2 11.2 %copy.38 = bf16[1,768,2048]{1,0,2:T(2,128)(2,1)} copy(bf16[1,768,2048]{2,1,0:T(8,128)(2,1)S(1)} %fusion.9) | data formatting | bytes 6291456 | tf_op jit(solution)/shard_map/broadcast_in_dim | solution.py:109
  701.5 0.5 broadcast.199
  702.0 33.6 %reduce.3 = bf16[2048,768]{1,0:T(8,128)(2,1)} reduce(bf16[2048,1,768]{2,1,0:T(2,128)(2,1)} %bitcast.72, bf16[]{:T(256)} %broadcast.199), dimensions={1}, to_apply=%bitcast.67.reduce_sub_computation | reduce | bytes 6291458
  735.5 4.6 reshape.141
  740.2 72.8 %all_to_all.31 = bf16[8,2,98304]{2,1,0:T(2,128)(2,1)} all-to-all(bf16[8,2,98304]{2,1,0:T(2,128)(2,1)S(1)} %reshape.141), channel_id=1, replica_groups=mesh['dp'=8,'rep'=4] {'dp'}, dimensions={0} | all-to-all | bytes 6291456 | tf_op jit(solution)/shard_map/all_to_all | solution.py:109
  813.0 7.8 reshape.142
  820.8 3.3 copy.40
  824.1 1.6 slice.46
  825.6 4.3 copy.39
  (40 shorter events, 0.5 us)
Async XLA Ops:
  6.5 166.0 %copy-start = (bf16[512,2048]{1,0:T(8,128)(2,1)S(1)}, bf16[512,2048]{1,0:T(8,128)(2,1)}, u32[]{:S(2)}) copy-start(bf16[512,2048]{1,0:T(8,128)(2,1)} %param.13) | copy-start | bytes 6291460
  6.5 490.8 %reduce-scatter.2.cloned.1.call-start = ((), (), s32[]{:S(2)}) async-start(), calls=%async_computation.3 | async-start | bytes 21233664 | tf_op jit(solution)/shard_map/reduce_scatter | solution.py:93
  6.5 23.8 %collective-permute-start = (bf16[2,768,256]{2,1,0:T(8,128)(2,1)}, bf16[2,768,256]{2,1,0:T(8,128)(2,1)S(1)}, u32[]{:S(2)}, u32[]{:S(2)}) collective-permute-start(bf16[2,768,256]{2,1,0:T(8,128)(2,1)} %param.17), channel_id=1, source_target_pairs={{0,4},{4,8},{8,12},{12,16},{16,20},{20,24},{24,28},{28,0},{1,5},{5... | collective-permute-start | bytes 2359304 | tf_op jit(solution)/shard_map/ppermute | solution.py:72
  30.3 21.4 %collective-permute-start.1 = (bf16[2,768,256]{2,1,0:T(8,128)(2,1)S(1)}, bf16[2,768,256]{2,1,0:T(8,128)(2,1)S(1)}, u32[]{:S(2)}, u32[]{:S(2)}) collective-permute-start(bf16[2,768,256]{2,1,0:T(8,128)(2,1)S(1)} %collective-permute-done), channel_id=1, source_target_pairs={{0,4},{4,8},{8,12},{12,16},{16,20},{20,24},{24,28},{28,0},{1,5},{5... | collective-permute-start | bytes 2359304 | tf_op jit(solution)/shard_map/ppermute | solution.py:72
  51.7 0.9 copy-start.4
  52.6 20.5 %collective-permute-start.2 = (bf16[2,768,256]{2,1,0:T(8,128)(2,1)S(1)}, bf16[2,768,256]{2,1,0:T(8,128)(2,1)S(1)}, u32[]{:S(2)}, u32[]{:S(2)}) collective-permute-start(bf16[2,768,256]{2,1,0:T(8,128)(2,1)S(1)} %collective-permute-done.1), channel_id=1, source_target_pairs={{0,4},{4,8},{8,12},{12,16},{16,20},{20,24},{24,28},{28,0},{1,5},{5... | collective-permute-start | bytes 2359304 | tf_op jit(solution)/shard_map/ppermute | solution.py:72
  73.1 0.9 copy-start.6
  74.0 19.7 %collective-permute-start.3 = (bf16[2,768,256]{2,1,0:T(8,128)(2,1)S(1)}, bf16[2,768,256]{2,1,0:T(8,128)(2,1)S(1)}, u32[]{:S(2)}, u32[]{:S(2)}) collective-permute-start(bf16[2,768,256]{2,1,0:T(8,128)(2,1)S(1)} %collective-permute-done.2), channel_id=1, source_target_pairs={{0,4},{4,8},{8,12},{12,16},{16,20},{20,24},{24,28},{28,0},{1,5},{5... | collective-permute-start | bytes 2359304 | tf_op jit(solution)/shard_map/ppermute | solution.py:72
  93.7 0.9 copy-start.8
  94.6 18.8 %collective-permute-start.4 = (bf16[2,768,256]{2,1,0:T(8,128)(2,1)S(1)}, bf16[2,768,256]{2,1,0:T(8,128)(2,1)S(1)}, u32[]{:S(2)}, u32[]{:S(2)}) collective-permute-start(bf16[2,768,256]{2,1,0:T(8,128)(2,1)S(1)} %collective-permute-done.3), channel_id=1, source_target_pairs={{0,4},{4,8},{8,12},{12,16},{16,20},{20,24},{24,28},{28,0},{1,5},{5... | collective-permute-start | bytes 2359304 | tf_op jit(solution)/shard_map/ppermute | solution.py:72
  113.4 0.9 copy-start.10
  114.3 18.1 %collective-permute-start.5 = (bf16[2,768,256]{2,1,0:T(8,128)(2,1)S(1)}, bf16[2,768,256]{2,1,0:T(8,128)(2,1)}, u32[]{:S(2)}, u32[]{:S(2)}) collective-permute-start(bf16[2,768,256]{2,1,0:T(8,128)(2,1)S(1)} %collective-permute-done.4), channel_id=1, source_target_pairs={{0,4},{4,8},{8,12},{12,16},{16,20},{20,24},{24,28},{28,0},{1,5},{5... | collective-permute-start | bytes 2359304 | tf_op jit(solution)/shard_map/ppermute | solution.py:72
  132.4 17.4 %collective-permute-start.6 = (bf16[2,768,256]{2,1,0:T(8,128)(2,1)}, bf16[2,768,256]{2,1,0:T(8,128)(2,1)}, u32[]{:S(2)}, u32[]{:S(2)}) collective-permute-start(bf16[2,768,256]{2,1,0:T(8,128)(2,1)} %collective-permute-done.5), channel_id=1, source_target_pairs={{0,4},{4,8},{8,12},{12,16},{16,20},{20,24},{24,28},{28,0},{1,5},{5... | collective-permute-start | bytes 2359304 | tf_op jit(solution)/shard_map/ppermute | solution.py:72
  135.0 17.4 %copy-start.11 = (bf16[2,768,256]{2,1,0:T(8,128)(2,1)S(1)}, bf16[2,768,256]{2,1,0:T(8,128)(2,1)}, u32[]{:S(2)}) copy-start(bf16[2,768,256]{2,1,0:T(8,128)(2,1)} %copy-done.10) | copy-start | bytes 2359300
  136.8 20.1 %copy-start.12 = (bf16[512,2048]{1,0:T(8,128)(2,1)}, bf16[512,2048]{1,0:T(8,128)(2,1)S(1)}, u32[]{:S(2)}) copy-start(bf16[512,2048]{1,0:T(8,128)(2,1)S(1)} %broadcast_select_fusion) | copy-start | bytes 6291460
  136.9 15.7 %copy-start.9 = (bf16[2,768,256]{2,1,0:T(8,128)(2,1)S(1)}, bf16[2,768,256]{2,1,0:T(8,128)(2,1)}, u32[]{:S(2)}) copy-start(bf16[2,768,256]{2,1,0:T(8,128)(2,1)} %copy-done.8) | copy-start | bytes 2359300
  136.9 15.8 %copy-start.7 = (bf16[2,768,256]{2,1,0:T(8,128)(2,1)S(1)}, bf16[2,768,256]{2,1,0:T(8,128)(2,1)}, u32[]{:S(2)}) copy-start(bf16[2,768,256]{2,1,0:T(8,128)(2,1)} %copy-done.6) | copy-start | bytes 2359300
  151.1 1.7 copy-start.5
  152.5 1.1 copy-start.3
  156.5 1.1 copy-start.14
  156.5 1.4 copy-start.15
  167.1 5.5 copy-start.13
  190.0 364.5 %all-reduce.3.cloned.1.call-start = ((), (), s32[]{:S(2)}) async-start(), calls=%async_computation.4 | async-start | bytes 4718592 | tf_op jit(solution)/shard_map/psum | solution.py:96
  554.5 23.8 %copy-start.2 = (bf16[2,3,768,256]{3,2,1,0:T(8,128)(2,1)S(1)}, bf16[2,3,768,256]{3,2,1,0:T(8,128)(2,1)}, u32[]{:S(2)}) copy-start(bf16[2,3,768,256]{3,2,1,0:T(8,128)(2,1)} %all-reduce.3.cloned.1.call-done) | copy-start | bytes 7077892
  824.1 5.8 copy-start.1
Sparse Core Ops, SparseCore 0:
  190.1 307.1 reduce-scatter.1
  499.7 54.7 all-reduce.2
